TPU v7x, 128 devices: a whole 4x4x4 slice. The times are simulated.
128 devices in a mesh: lat: 8 (over y, x_hi), lon: 16 (over x_lo, z, core).
Axes of the slice: x: 4 (x_hi: 2, x_lo: 2; x = x_hi * 2 + x_lo), y: 4, z: 4, core: 2. Of those that a mesh axis runs over, the one named last changes fastest.
Arguments:
- adjoint_in: float32 [4, 79, 64, 2048], P(None, None, 'lat', 'lon'), may hold values from -6 to 6
- fractions: bfloat16 [4, 4, 79, 64, 2048], P(None, None, None, 'lat', 'lon'), may hold values from 0 to 0.95, as said below
- profiles: bfloat16 [2, 79, 64, 2048], P(None, None, 'lat', 'lon'), may hold values from 0.099609375 to 1
- kernel: bfloat16 [79, 79], replicated, may hold values from -0.625 to 0.625
- obs_weights: bfloat16 [79, 524288], P(None, ('lat', 'lon')), may hold values from 0.099609375 to 1.5
- obs_resid: bfloat16 [4, 524288], P(None, ('lat', 'lon')), may hold values from -5 to 5
- obs_cols: int32 [524288], P(('lat', 'lon')), may hold values from 0 to 1023
- obs_owner: int32 [65536, 1], P(('lat', 'lon')), may hold values from 0 to 127; in each aligned block of 512 rows (0 to 511, 512 to 1023, ...) at most 6 rows name the same one
- obs_count: int32 [65536], P(('lat', 'lon')), may hold values from 5 to 8
- lat_matrix: bfloat16 [64, 64], replicated, as said below
- lon_matrix: bfloat16 [2048, 2048], P('lon'), as said below
Outputs:
- adjoint_out: float32 [4, 79, 64, 2048], P(None, None, 'lat', 'lon')
- smoothed_gradient: float32 [4, 64, 2048], P(None, 'lat', 'lon')
Inputs may be any that keep to these rules, and one draw needn't show every extreme that they name: `fractions`: fractions are nonnegative and the four of one cell and step sum to at most 0.95. `obs_owner`: owners are numbered as lat index times 16 plus lon index. Among the blocks of one device at most 6 share an owner. `obs_cols`: A tile's columns are numbered row by row: row within the tile times 128 plus column within the tile. The first obs_count slots of a block are valid, the others are padding. `lat_matrix`: Symmetric. `lon_matrix`: Symmetric.
All inputs are finite; a program needn't handle non-finite values.
Results may differ from a plain program's by a relative error of at most 0.0041.
Values may be sent and summed in bfloat16 or wider, within the bound.
A program may use at most 192 MiB of HBM per device.

v0:
```python
import functools

import jax
import jax.numpy as jnp
from jax import lax
from jax.experimental import pallas as pl
from jax.experimental.pallas import tpu as pltpu
from jax.sharding import PartitionSpec as P

STEPS = 4
CAPACITY = 6
SLOTS = 8
MESH = pl.DeviceIdType.MESH
F32 = jnp.float32
BF16 = jnp.bfloat16
VMEM = pl.BlockSpec(memory_space=pltpu.VMEM)
SMEM = pl.BlockSpec(memory_space=pltpu.SMEM)


def padded(levels):
    return -(-levels // 16) * 16


def pack_kernel(levels, tracers, devices, w_ref, r_ref, c_ref, owner_ref, count_ref, out_ref, feat, rows, seen):
    blocks = owner_ref.shape[0]
    lanes = 128
    per_chunk = lanes // SLOTS
    feat[0:levels, :] = w_ref[...].astype(F32)
    feat[levels : levels + tracers, :] = r_ref[...].astype(F32)
    cell = c_ref[...]
    feat[levels + tracers : levels + tracers + 1, :] = (cell // lanes).astype(F32)
    feat[levels + tracers + 1 : levels + tracers + 2, :] = (cell % lanes).astype(F32)
    rows[...] = jnp.zeros_like(rows)

    @pl.loop(0, devices)
    def _(d):
        seen[d] = 0

    slot = lax.broadcasted_iota(jnp.int32, (SLOTS, lanes), 0)

    @pl.loop(0, blocks // per_chunk)
    def _(chunk):
        at = pl.multiple_of(chunk * lanes, lanes)
        turned = feat[:, pl.ds(at, lanes)].T
        for i in range(per_chunk):
            b = chunk * per_chunk + i
            owner = owner_ref[b]
            rank = seen[owner]
            seen[owner] = rank + 1
            place = pl.multiple_of((owner * CAPACITY + rank) * SLOTS, SLOTS)
            block = turned[i * SLOTS : (i + 1) * SLOTS, :]
            rows[pl.ds(place, SLOTS), :] = jnp.where(slot < count_ref[b], block, 0.0)

    width = levels + tracers + 2
    spare = lanes - width
    lane = lax.broadcasted_iota(jnp.int32, (SLOTS, lanes), 1)

    @pl.loop(0, devices, unroll=4)
    def _(d):
        base = d * (CAPACITY * SLOTS)
        got = [rows[pl.ds(pl.multiple_of(base + i * SLOTS, SLOTS), SLOTS), :] for i in range(CAPACITY)]
        pieces = []
        for i in range(4):
            extra = got[4 + i // 2]
            shift = width if i % 2 == 0 else width - spare
            pieces.append(jnp.where(lane < width, got[i], pltpu.roll(extra, shift, 1)))
        out_ref[d] = jnp.concatenate(pieces, axis=0).astype(BF16)


def steps_kernel(
    tracers, levels, lat_rows,
    adj_ref, frac_ref, prof_ref, ker_ref,
    state, surf_ref,
    mixed, fracs, profs, square,
    lat_send, lat_recv, lon_send, lon_recv,
    lat_ss, lat_rs, lon_ss, lon_rs,
):
    lanes = 128
    lev = padded(levels)
    rows = levels * lat_rows
    lat, lon = lax.axis_index("lat"), lax.axis_index("lon")
    nlat, nlon = lax.axis_size("lat"), lax.axis_size("lon")
    up, down = lax.rem(lat + 1, nlat), lax.rem(lat + nlat - 1, nlat)
    east, west = lax.rem(lon + 1, nlon), lax.rem(lon + nlon - 1, nlon)
    barrier = pltpu.get_barrier_semaphore()
    pl.semaphore_signal(barrier, inc=1, device_id={"lat": up}, device_id_type=MESH)
    pl.semaphore_signal(barrier, inc=1, device_id={"lat": down}, device_id_type=MESH)
    pl.semaphore_signal(barrier, inc=1, device_id={"lon": east}, device_id_type=MESH)
    pl.semaphore_signal(barrier, inc=1, device_id={"lon": west}, device_id_type=MESH)

    @pl.when(lat == 0)
    def _():
        for n in range(STEPS):
            lat_recv[n, 0] = jnp.zeros((lev, tracers * lanes), BF16)

    @pl.when(lat == nlat - 1)
    def _():
        for n in range(STEPS):
            lat_recv[n, 1] = jnp.zeros((lev, tracers * lanes), BF16)

    square[...] = jnp.zeros_like(square)
    square[0:levels, 0:levels] = ker_ref[...].astype(F32)
    turned = square[...].T[0:lev, 0:lev].astype(BF16)
    pad = lev * lat_rows - rows
    for i in range(2):
        profs[i, 0:rows, :] = prof_ref[i * rows : (i + 1) * rows, :].astype(F32)
        profs[i, rows : rows + pad, :] = jnp.zeros((pad, lanes), F32)
    for f in range(4):
        fracs[f, rows : rows + pad, :] = jnp.zeros((pad, lanes), F32)
    for y in range(lat_rows):
        state[y, levels:lev, :] = jnp.zeros((lev - levels, tracers * lanes), F32)
        for t in range(tracers):
            state[y, 0:levels, t * lanes : (t + 1) * lanes] = adj_ref[pl.ds(t * rows + y, levels, stride=lat_rows), :]
    surf_ref[...] = jnp.zeros_like(surf_ref)
    pl.semaphore_wait(barrier, 4)

    lane = lax.broadcasted_iota(jnp.int32, (lev, lanes), 1)
    half = lev // 2
    lane_half = lax.broadcasted_iota(jnp.int32, (half, lanes), 1)

    def lat_copy(i, side):
        return pltpu.make_async_remote_copy(
            src_ref=lat_send.at[i, side],
            dst_ref=lat_recv.at[i, 1 - side],
            send_sem=lat_ss.at[i, side],
            recv_sem=lat_rs.at[i, 1 - side],
            device_id={"lat": up if side else down},
            device_id_type=MESH,
        )

    def lon_copy(i, side):
        return pltpu.make_async_remote_copy(
            src_ref=lon_send.at[i, side],
            dst_ref=lon_recv.at[i, 1 - side],
            send_sem=lon_ss.at[i, side],
            recv_sem=lon_rs.at[i, 1 - side],
            device_id={"lon": east if side else west},
            device_id_type=MESH,
        )

    def step(i, _):
        n = STEPS - 1 - i
        columns = [jnp.zeros((lev, lanes), F32), jnp.zeros((lev, lanes), F32)]
        order = [0, lat_rows - 1] + list(range(1, lat_rows - 1))
        for y in order:
            entrain = profs[0, pl.ds(y, lev, stride=lat_rows), :]
            detrain = profs[1, pl.ds(y, lev, stride=lat_rows), :]
            lowered = (jnp.concatenate([detrain] * tracers, axis=1) * state[y]).astype(BF16)
            mixing = jnp.dot(turned, lowered, preferred_element_type=F32)
            mixed[y] = state[y] + jnp.concatenate([entrain] * tracers, axis=1) * mixing
            if y == 0:
                lat_send[i, 0] = mixed[y].astype(BF16)

                @pl.when(lat > 0)
                def _():
                    lat_copy(i, 0).start()

            if y == lat_rows - 1:
                lat_send[i, 1] = mixed[y].astype(BF16)

                @pl.when(lat < nlat - 1)
                def _():
                    lat_copy(i, 1).start()

        for y in range(lat_rows):
            for t in range(tracers):
                at = y * tracers + t
                tile = mixed[y, :, t * lanes : (t + 1) * lanes]
                west_edge = tile if at == 0 else pltpu.roll(tile, at, 1)
                columns[0] = jnp.where(lane == at, west_edge, columns[0])
                columns[1] = jnp.where(lane == at, pltpu.roll(tile, at + 1, 1), columns[1])
        for side in range(2):
            lon_send[i, side] = columns[side]
            lon_copy(i, side).start()
        for f in range(4):
            at = pl.multiple_of((n * 4 + f) * rows, 8)
            fracs[f, 0:rows, :] = frac_ref[pl.ds(at, rows), :].astype(F32)
        lon_copy(i, 0).wait_recv()
        lon_copy(i, 1).wait_recv()

        def advance(y):
            for h in range(2):
                ks = slice(h * half, (h + 1) * half)
                f = [fracs[j, pl.ds(h * half * lat_rows + y, half, stride=lat_rows), :] for j in range(4)]
                remain = 1.0 - f[0] - f[1] - f[2] - f[3]
                from_west, from_east = lon_recv[i, 0, ks, :], lon_recv[i, 1, ks, :]
                for t in range(tracers):
                    ts = slice(t * lanes, (t + 1) * lanes)
                    at = y * tracers + t
                    here = mixed[y, ks, ts]
                    side_e = jnp.where(
                        lane_half == lanes - 1,
                        jnp.broadcast_to(from_east[:, at : at + 1], (half, lanes)),
                        pltpu.roll(here, lanes - 1, 1),
                    )
                    side_w = jnp.where(
                        lane_half == 0,
                        jnp.broadcast_to(from_west[:, at : at + 1], (half, lanes)),
                        pltpu.roll(here, 1, 1),
                    )
                    north = lat_recv[i, 1, ks, ts].astype(F32) if y == lat_rows - 1 else mixed[y + 1, ks, ts]
                    south = lat_recv[i, 0, ks, ts].astype(F32) if y == 0 else mixed[y - 1, ks, ts]
                    state[y, ks, ts] = remain * here + f[0] * side_e + f[1] * side_w + f[2] * north + f[3] * south

        for y in range(1, lat_rows - 1):
            advance(y)

        @pl.when(lat < nlat - 1)
        def _():
            lat_copy(i, 0).wait_recv()

        @pl.when(lat > 0)
        def _():
            lat_copy(i, 1).wait_recv()

        advance(0)
        advance(lat_rows - 1)

        @pl.when(i < STEPS - 1)
        def _():
            for y in range(lat_rows):
                surf_ref[y] += state[y, 0:8, :]

        return 0

    lax.fori_loop(0, STEPS, step, 0)
    for i in range(STEPS):
        for side in range(2):
            lon_copy(i, side).wait_send()

        @pl.when(lat > 0)
        def _():
            lat_copy(i, 0).wait_send()

        @pl.when(lat < nlat - 1)
        def _():
            lat_copy(i, 1).wait_send()


def forcing_kernel(tracers, levels, lat_rows, group, recv_ref, state_ref, surf_ref, out_ref, low_ref, acc, rows, lhs, rhs, flat):
    lanes = 128
    lev = padded(levels)
    devices = recv_ref.shape[0]
    width = levels + tracers + 2
    spare = lanes - width
    slots = CAPACITY * SLOTS
    acc[...] = state_ref[...].reshape(acc.shape)
    lane8 = lax.broadcasted_iota(jnp.int32, (SLOTS, lanes), 1)
    lane16 = lax.broadcasted_iota(jnp.int32, (16, lanes), 1).astype(F32)

    @pl.loop(0, devices // group)
    def _(g):
        for p in range(group):
            block = recv_ref[g * group + p].astype(F32)
            quarter = [block[i * SLOTS : (i + 1) * SLOTS] for i in range(4)]
            for i in range(4):
                rows[p * slots + i * SLOTS : p * slots + (i + 1) * SLOTS, :] = quarter[i]
            for i in range(2):
                low = pltpu.roll(quarter[2 * i], lanes - width, 1)
                high = pltpu.roll(quarter[2 * i + 1], lanes - width + spare, 1)
                at = p * slots + (4 + i) * SLOTS
                rows[at : at + SLOTS, :] = jnp.where(lane8 < spare, low, high)
        for c in range(group * slots // lanes):
            turned = rows[c * lanes : (c + 1) * lanes, :].T
            weights = turned[0:lev, :]
            row = turned[levels + tracers : levels + tracers + 1, :]
            for y in range(lat_rows):
                lhs[y * lev : (y + 1) * lev, c * lanes : (c + 1) * lanes] = jnp.where(row == y, weights, 0.0).astype(BF16)
        for s in range(group * slots // 16):
            here = rows[s * 16 : (s + 1) * 16, :]
            col = jnp.broadcast_to(here[:, width - 1 : width], (16, lanes)) == lane16
            for t in range(tracers):
                value = jnp.broadcast_to(here[:, levels + t : levels + t + 1], (16, lanes))
                rhs[s * 16 : (s + 1) * 16, t * lanes : (t + 1) * lanes] = jnp.where(col, value, 0.0).astype(BF16)
        acc[...] += jnp.dot(lhs[...], rhs[...], preferred_element_type=F32)

    for y in range(lat_rows):
        for t in range(tracers):
            ts = slice(t * lanes, (t + 1) * lanes)
            out_ref[pl.ds(t * levels * lat_rows + y, levels, stride=lat_rows), :] = acc[y * lev : y * lev + levels, ts]
            at = y * tracers + t
            flat[at : at + 1, :] = surf_ref[y, 0:1, ts] + acc[y * lev : y * lev + 1, ts]
    low_ref[...] = flat[...].astype(BF16)


def smooth_kernel(tracers, lat_rows, low_ref, lonm_ref, latm_ref, out_ref, lon_got, lat_got, own, ss_lon, rs_lon, ss_lat, rs_lat):
    lanes = 128
    lat, lon = lax.axis_index("lat"), lax.axis_index("lon")
    nlat, nlon = lax.axis_size("lat"), lax.axis_size("lon")
    rows = tracers * lat_rows
    barrier = pltpu.get_barrier_semaphore()
    for d in range(1, nlon):
        pl.semaphore_signal(barrier, inc=1, device_id={"lon": lax.rem(lon + d, nlon)}, device_id_type=MESH)
    for d in range(1, nlat):
        pl.semaphore_signal(barrier, inc=1, device_id={"lat": lax.rem(lat + d, nlat)}, device_id_type=MESH)
    pl.semaphore_wait(barrier, nlon + nlat - 2)

    def lon_copy(d):
        return pltpu.make_async_remote_copy(
            src_ref=low_ref, dst_ref=lon_got.at[d], send_sem=ss_lon.at[d], recv_sem=rs_lon.at[d],
            device_id={"lon": lax.rem(lon + d, nlon)}, device_id_type=MESH,
        )

    def lat_copy(d):
        return pltpu.make_async_remote_copy(
            src_ref=own, dst_ref=lat_got.at[d], send_sem=ss_lat.at[d], recv_sem=rs_lat.at[d],
            device_id={"lat": lax.rem(lat + d, nlat)}, device_id_type=MESH,
        )

    for d in range(1, nlon):
        lon_copy(d).start()

    nrow = latm_ref.shape[0]
    pick = lax.broadcasted_iota(jnp.int32, (rows, nrow), 1) == lat * lat_rows + lax.broadcasted_iota(
        jnp.int32, (rows, nrow), 0
    ) % lat_rows
    own_rows = jnp.dot(jnp.where(pick, 1.0, 0.0).astype(BF16), latm_ref[...], preferred_element_type=F32).astype(BF16)
    spread = lax.broadcasted_iota(jnp.int32, (nrow, nrow * tracers), 0) == lax.broadcasted_iota(
        jnp.int32, (nrow, nrow * tracers), 1
    ) // tracers
    wide = jnp.dot(own_rows, jnp.where(spread, 1.0, 0.0).astype(BF16), preferred_element_type=F32)
    same = lax.broadcasted_iota(jnp.int32, (rows, nrow * tracers), 0) // lat_rows == lax.broadcasted_iota(
        jnp.int32, (rows, nrow * tracers), 1
    ) % tracers
    wide = jnp.where(same, wide, 0.0)

    contract = (((1,), (1,)), ((), ()))

    def part(d, block):
        source = lax.rem(lon - d + nlon, nlon)
        matrix = lonm_ref[:, pl.ds(pl.multiple_of(source * lanes, lanes), lanes)]
        return lax.dot_general(block, matrix, contract, preferred_element_type=F32)

    total = part(0, low_ref[...])
    for d in range(1, nlon):
        lon_copy(d).wait_recv()
        total += part(d, lon_got[d])
    own[...] = total.astype(BF16)
    for d in range(1, nlat):
        lat_copy(d).start()
    lat_got[0] = own[...]
    blocks = []
    for d in range(nlat):
        if d:
            lat_copy(d).wait_recv()
        blocks.append(lat_got[d])
    gathered = jnp.concatenate(blocks, axis=0)
    turned = pltpu.roll(wide, (nlat - 1 - lat) * rows, 1)
    reordered = jnp.concatenate(
        [turned[:, (nlat - 1 - d) * rows : (nlat - d) * rows] for d in range(nlat)], axis=1
    ).astype(BF16)
    smoothed = jnp.dot(reordered, gathered, preferred_element_type=F32)
    out_ref[...] = smoothed.reshape(out_ref.shape)
    for d in range(1, nlon):
        lon_copy(d).wait_send()
    for d in range(1, nlat):
        lat_copy(d).wait_send()


def shards(
    adjoint_in, fractions, profiles, kernel, obs_weights, obs_resid, obs_cols, obs_owner, obs_count, lat_matrix, lon_matrix
):
    tracers, levels, lat_rows, lanes = adjoint_in.shape
    lev = padded(levels)
    nlat, nlon = lax.axis_size("lat"), lax.axis_size("lon")
    devices = nlat * nlon
    blocks = obs_count.shape[0]
    nslots = blocks * SLOTS
    big = dict(vmem_limit_bytes=60 << 20)

    packed = pl.pallas_call(
        functools.partial(pack_kernel, levels, tracers, devices),
        out_shape=jax.ShapeDtypeStruct((devices, 4 * SLOTS, lanes), BF16),
        in_specs=[VMEM, VMEM, VMEM, SMEM, SMEM],
        out_specs=VMEM,
        scratch_shapes=[
            pltpu.VMEM((lanes, nslots), F32),
            pltpu.VMEM((devices * CAPACITY * SLOTS, lanes), F32),
            pltpu.SMEM((devices,), jnp.int32),
        ],
        compiler_params=pltpu.CompilerParams(**big),
        name="pack",
    )(obs_weights, obs_resid, obs_cols.reshape(1, nslots), obs_owner.reshape(blocks), obs_count)
    received = lax.all_to_all(packed, ("lat", "lon"), 0, 0, tiled=True)

    rows = levels * lat_rows
    state, surface = pl.pallas_call(
        functools.partial(steps_kernel, tracers, levels, lat_rows),
        out_shape=(
            jax.ShapeDtypeStruct((lat_rows, lev, tracers * lanes), F32),
            jax.ShapeDtypeStruct((lat_rows, 8, tracers * lanes), F32),
        ),
        in_specs=[VMEM] * 4,
        out_specs=(VMEM, VMEM),
        scratch_shapes=[
            pltpu.VMEM((lat_rows, lev, tracers * lanes), F32),
            pltpu.VMEM((4, lev * lat_rows, lanes), F32),
            pltpu.VMEM((2, lev * lat_rows, lanes), F32),
            pltpu.VMEM((lanes, lanes), F32),
            pltpu.VMEM((STEPS, 2, lev, tracers * lanes), BF16),
            pltpu.VMEM((STEPS, 2, lev, tracers * lanes), BF16),
            pltpu.VMEM((STEPS, 2, lev, lanes), F32),
            pltpu.VMEM((STEPS, 2, lev, lanes), F32),
            pltpu.SemaphoreType.DMA((STEPS, 2)),
            pltpu.SemaphoreType.DMA((STEPS, 2)),
            pltpu.SemaphoreType.DMA((STEPS, 2)),
            pltpu.SemaphoreType.DMA((STEPS, 2)),
        ],
        compiler_params=pltpu.CompilerParams(collective_id=0, has_side_effects=True, **big),
        name="steps",
    )(
        adjoint_in.reshape(tracers * rows, lanes),
        fractions.reshape(STEPS * 4 * rows, lanes),
        profiles.reshape(2 * rows, lanes),
        kernel,
    )

    group = min(16, devices)
    adjoint, low = pl.pallas_call(
        functools.partial(forcing_kernel, tracers, levels, lat_rows, group),
        out_shape=(
            jax.ShapeDtypeStruct((tracers * rows, lanes), F32),
            jax.ShapeDtypeStruct((lat_rows * tracers, lanes), BF16),
        ),
        in_specs=[VMEM] * 3,
        out_specs=(VMEM, VMEM),
        scratch_shapes=[
            pltpu.VMEM((lat_rows * lev, tracers * lanes), F32),
            pltpu.VMEM((group * CAPACITY * SLOTS, lanes), F32),
            pltpu.VMEM((lat_rows * lev, group * CAPACITY * SLOTS), BF16),
            pltpu.VMEM((group * CAPACITY * SLOTS, tracers * lanes), BF16),
            pltpu.VMEM((lat_rows * tracers, lanes), F32),
        ],
        compiler_params=pltpu.CompilerParams(**big),
        name="forcing",
    )(received, state, surface)

    smoothed = pl.pallas_call(
        functools.partial(smooth_kernel, tracers, lat_rows),
        out_shape=jax.ShapeDtypeStruct((tracers, lat_rows, lanes), F32),
        in_specs=[VMEM] * 3,
        out_specs=VMEM,
        scratch_shapes=[
            pltpu.VMEM((nlon, lat_rows * tracers, lanes), BF16),
            pltpu.VMEM((nlat, lat_rows * tracers, lanes), BF16),
            pltpu.VMEM((lat_rows * tracers, lanes), BF16),
            pltpu.SemaphoreType.DMA((nlon,)),
            pltpu.SemaphoreType.DMA((nlon,)),
            pltpu.SemaphoreType.DMA((nlat,)),
            pltpu.SemaphoreType.DMA((nlat,)),
        ],
        compiler_params=pltpu.CompilerParams(collective_id=1, has_side_effects=True, **big),
        name="smooth",
    )(low, lon_matrix, lat_matrix)
    return adjoint.reshape(adjoint_in.shape), smoothed


def solution(mesh):
    placed = (
        P(None, None, "lat", "lon"),
        P(None, None, None, "lat", "lon"),
        P(None, None, "lat", "lon"),
        P(),
        P(None, ("lat", "lon")),
        P(None, ("lat", "lon")),
        P(("lat", "lon")),
        P(("lat", "lon"), None),
        P(("lat", "lon")),
        P(),
        P("lon", None),
    )
    return jax.shard_map(
        shards,
        mesh=mesh,
        in_specs=placed,
        out_specs=(P(None, None, "lat", "lon"), P(None, "lat", "lon")),
        check_vma=False,
    )
```

profile of v0, /device:TPU:1, one launch (start us, length us, event | category | flops | bytes accessed | tf_op | source)
XLA Modules:
  0.0 95.5 jit_solution(8589621173100698408)
XLA Ops:
  0.6 9.0 %pack.1 = bf16[128,32,128]{2,1,0:T(8,128)(2,1)} custom-call(bf16[79,4096]{1,0:T(8,128)(2,1)} %w_ref.1, bf16[4,4096]{1,0:T(4,128)(2,1)} %r_ref.1, s32[1,4096]{1,0:T(1,128)} %bitcast.9, s32[512]{0:T(512)} %bitcast.10, s32[512]{0:T(512)} %count_ref.1), custom_call_target="tpu_custom_call" | custom-call | tf_op jit(solution)/shard_map/pack/pallas_call | solution.py:371
  9.7 11.5 %all-to-all-start = ((bf16[128,32,128]{2,1,0:T(8,128)(2,1)}), bf16[128,32,128]{2,1,0:T(8,128)(2,1)S(1)}, u32[]{:S(2)}, u32[]{:S(2)}) async-start(bf16[128,32,128]{2,1,0:T(8,128)(2,1)} %pack.1), calls=%async_computation | async-start | bytes 2097152 | tf_op jit(solution)/shard_map/all_to_all | solution.py:384
  21.1 39.9 %steps.1 = (f32[8,80,512]{2,1,0:T(8,128)}, f32[8,8,512]{2,1,0:T(8,128)}) custom-call(f32[2528,128]{1,0:T(8,128)} %bitcast.7, bf16[10112,128]{1,0:T(8,128)(2,1)} %bitcast.6, bf16[1264,128]{1,0:T(8,128)(2,1)} %bitcast.8, bf16[79,79]{1,0:T(8,128)(2,1)} %ker_ref.1), custom_call_target="tpu_custom_call" | custom-call | tf_op jit(solution)/shard_map/steps/pallas_call | solution.py:387
  61.0 0.0 all-to-all-done.recv_ref
  61.0 0.0 copy-start
  61.0 1.0 %copy-done = bf16[128,32,128]{2,1,0:T(8,128)(2,1)} copy-done((bf16[128,32,128]{2,1,0:T(8,128)(2,1)}, bf16[128,32,128]{2,1,0:T(8,128)(2,1)S(1)}, u32[]{:S(2)}) %copy-start) | copy-done | bytes 1048600
  62.0 12.0 %forcing.1 = (f32[2528,128]{1,0:T(8,128)}, bf16[32,128]{1,0:T(8,128)(2,1)}) custom-call(bf16[128,32,128]{2,1,0:T(8,128)(2,1)} %copy-done, f32[8,80,512]{2,1,0:T(8,128)} %get-tuple-element.6.state_ref, f32[8,8,512]{2,1,0:T(8,128)} %get-tuple-element.7.surf_ref), custom_call_target="tpu_custom_call" | custom-call | tf_op jit(solution)/shard_map/forcing/pallas_call | solution.py:419
  74.0 20.2 %smooth.1 = f32[4,8,128]{2,1,0:T(8,128)} custom-call(bf16[32,128]{1,0:T(8,128)(2,1)} %get-tuple-element.9.low_ref, bf16[128,2048]{1,0:T(8,128)(2,1)} %lonm_ref.1, bf16[64,64]{1,0:T(8,128)(2,1)} %latm_ref.1), custom_call_target="tpu_custom_call" | custom-call | tf_op jit(solution)/shard_map/smooth/pallas_call | solution.py:438
  94.2 1.3 %copy.14 = f32[4,8,128]{2,1,0:T(8,128)} copy(f32[4,8,128]{2,1,0:T(8,128)} %smooth.1) | data formatting | bytes 32768
Async XLA Ops:
  9.7 51.4 %all-to-all-start = ((bf16[128,32,128]{2,1,0:T(8,128)(2,1)}), bf16[128,32,128]{2,1,0:T(8,128)(2,1)S(1)}, u32[]{:S(2)}, u32[]{:S(2)}) async-start(bf16[128,32,128]{2,1,0:T(8,128)(2,1)} %pack.1), calls=%async_computation | async-start | bytes 2097152 | tf_op jit(solution)/shard_map/all_to_all | solution.py:384
  61.0 1.0 %copy-start = (bf16[128,32,128]{2,1,0:T(8,128)(2,1)}, bf16[128,32,128]{2,1,0:T(8,128)(2,1)S(1)}, u32[]{:S(2)}) copy-start(bf16[128,32,128]{2,1,0:T(8,128)(2,1)S(1)} %all-to-all-done.recv_ref) | copy-start | bytes 3145732
where the time goes:
time: 95.8 us; the launch traced here: 95.5 us
  Pallas kernels  81.1 us (85%)
  starting transfers between devices  11.5 us (12%)
  local copies, waits for them, and re-layouts  2.3 us (2%)
    pallas_call x1, Pallas kernels, shards(): pl.pallas_call(functools.partial(steps_kernel, tracers, levels, lat_rows)...  39.9 us
    pallas_call x1, Pallas kernels, shards(): pl.pallas_call(functools.partial(smooth_kernel, tracers, lat_rows), out_s...  20.2 us
    pallas_call x1, Pallas kernels, shards(): pl.pallas_call(functools.partial(forcing_kernel, tracers, levels, lat_row...  12 us
    all_to_all x1, starting transfers between devices, shards(): received = lax.all_to_all(packed, ('lat', 'lon'), 0, 0, tiled=True)  11.5 us
    pallas_call x1, Pallas kernels, shards(): pl.pallas_call(functools.partial(pack_kernel, levels, tracers, devices),...  9.02 us
    unnamed x3, local copies, waits for them, and re-layouts  2.3 us
  transfers between devices with their start and end apart: 1, of which 0 were waited for; matrix products, arithmetic and copies ran while one was open for 0% of the time, Pallas kernels for 42%

commit v1 on v0

v1 whole, which is shorter than its diff:
```python
import functools

import jax
import jax.numpy as jnp
from jax import lax
from jax.experimental import pallas as pl
from jax.experimental.pallas import tpu as pltpu
from jax.sharding import PartitionSpec as P

STEPS = 4
CAPACITY = 6
SLOTS = 8
CHAINS = 2
MESH = pl.DeviceIdType.MESH
F32 = jnp.float32
BF16 = jnp.bfloat16
VMEM = pl.BlockSpec(memory_space=pltpu.VMEM)
SMEM = pl.BlockSpec(memory_space=pltpu.SMEM)


def padded(levels):
    return -(-levels // 16) * 16


def pack_kernel(levels, tracers, devices, w_ref, r_ref, c_ref, owner_ref, count_ref, out_ref, feat, rows, seen):
    blocks = owner_ref.shape[0]
    lanes = 128
    per_chunk = lanes // SLOTS
    feat[0:levels, :] = w_ref[...].astype(F32)
    feat[levels : levels + tracers, :] = r_ref[...].astype(F32)
    cell = c_ref[...]
    feat[levels + tracers : levels + tracers + 1, :] = (cell // lanes).astype(F32)
    feat[levels + tracers + 1 : levels + tracers + 2, :] = (cell % lanes).astype(F32)
    rows[...] = jnp.zeros_like(rows)

    @pl.loop(0, devices)
    def _(d):
        seen[d] = 0

    slot = lax.broadcasted_iota(jnp.int32, (SLOTS, lanes), 0)

    @pl.loop(0, blocks // per_chunk)
    def _(chunk):
        at = pl.multiple_of(chunk * lanes, lanes)
        turned = feat[:, pl.ds(at, lanes)].T
        for i in range(per_chunk):
            b = chunk * per_chunk + i
            owner = owner_ref[b]
            rank = seen[owner]
            seen[owner] = rank + 1
            place = pl.multiple_of((owner * CAPACITY + rank) * SLOTS, SLOTS)
            block = turned[i * SLOTS : (i + 1) * SLOTS, :]
            rows[pl.ds(place, SLOTS), :] = jnp.where(slot < count_ref[b], block, 0.0)

    width = levels + tracers + 2
    spare = lanes - width
    lane = lax.broadcasted_iota(jnp.int32, (SLOTS, lanes), 1)

    @pl.loop(0, devices, unroll=4)
    def _(d):
        base = d * (CAPACITY * SLOTS)
        got = [rows[pl.ds(pl.multiple_of(base + i * SLOTS, SLOTS), SLOTS), :] for i in range(CAPACITY)]
        pieces = []
        for i in range(4):
            extra = got[4 + i // 2]
            shift = width if i % 2 == 0 else width - spare
            pieces.append(jnp.where(lane < width, got[i], pltpu.roll(extra, shift, 1)))
        out_ref[d] = jnp.concatenate(pieces, axis=0).astype(BF16)


def exchange_kernel(
    tracers, levels, lat_rows, group,
    adj_ref, frac_ref, prof_ref, ker_ref, packed_ref, lonm_ref, latm_ref,
    out_ref, smooth_ref,
    state, surf_ref, mixed, fracs, profs, square,
    lat_send, lat_recv, lon_send, lon_recv,
    lat_ss, lat_rs, lon_ss, lon_rs,
    got, acc, slots, lhs, rhs, flat, low_ref, own_ref, lon_got, lat_got,
    all_ss, all_rs, ss_lon, rs_lon, ss_lat, rs_lat,
):
    lanes = 128
    lev = padded(levels)
    rows = levels * lat_rows
    lat, lon = lax.axis_index("lat"), lax.axis_index("lon")
    nlat, nlon = lax.axis_size("lat"), lax.axis_size("lon")
    up, down = lax.rem(lat + 1, nlat), lax.rem(lat + nlat - 1, nlat)
    east, west = lax.rem(lon + 1, nlon), lax.rem(lon + nlon - 1, nlon)
    devices = nlat * nlon
    me = lat * nlon + lon
    barrier = pltpu.get_barrier_semaphore()

    def place(d):
        to = lax.rem(me + d, devices)
        return to, {"lat": to // nlon, "lon": lax.rem(to, nlon)}

    @pl.loop(1, devices)
    def _(d):
        pl.semaphore_signal(barrier, inc=1, device_id=place(d)[1], device_id_type=MESH)

    @pl.when(lat == 0)
    def _():
        for n in range(STEPS):
            for c in range(CHAINS):
                lat_recv[n, c, 0] = jnp.zeros((lev, tracers // CHAINS * lanes), BF16)

    @pl.when(lat == nlat - 1)
    def _():
        for n in range(STEPS):
            for c in range(CHAINS):
                lat_recv[n, c, 1] = jnp.zeros((lev, tracers // CHAINS * lanes), BF16)

    square[...] = jnp.zeros_like(square)
    square[0:levels, 0:levels] = ker_ref[...].astype(F32)
    turned = square[...].T[0:lev, 0:lev].astype(BF16)
    pad = lev * lat_rows - rows
    for i in range(2):
        profs[i, 0:rows, :] = prof_ref[i * rows : (i + 1) * rows, :].astype(F32)
        profs[i, rows : rows + pad, :] = jnp.zeros((pad, lanes), F32)
    for f in range(4):
        fracs[f, rows : rows + pad, :] = jnp.zeros((pad, lanes), F32)
    for y in range(lat_rows):
        state[y, levels:lev, :] = jnp.zeros((lev - levels, tracers * lanes), F32)
        for t in range(tracers):
            state[y, 0:levels, t * lanes : (t + 1) * lanes] = adj_ref[pl.ds(t * rows + y, levels, stride=lat_rows), :]
    surf_ref[...] = jnp.zeros_like(surf_ref)
    acc[...] = jnp.zeros_like(acc)
    pl.semaphore_wait(barrier, devices - 1)

    def all_copy(d):
        to, where = place(d)
        return pltpu.make_async_remote_copy(
            src_ref=packed_ref.at[to], dst_ref=got.at[d], send_sem=all_ss.at[d], recv_sem=all_rs.at[d],
            device_id=where, device_id_type=MESH,
        )

    def send_all():
        @pl.loop(1, devices)
        def _(d):
            all_copy(d).start()

    got[0] = packed_ref[me]

    lane = lax.broadcasted_iota(jnp.int32, (lev, lanes), 1)
    half = lev // 2
    lane_half = lax.broadcasted_iota(jnp.int32, (half, lanes), 1)
    each = tracers // CHAINS
    wide = each * lanes

    def lat_copy(i, c, side):
        return pltpu.make_async_remote_copy(
            src_ref=lat_send.at[i, c, side],
            dst_ref=lat_recv.at[i, c, 1 - side],
            send_sem=lat_ss.at[i, c, side],
            recv_sem=lat_rs.at[i, c, 1 - side],
            device_id={"lat": up if side else down},
            device_id_type=MESH,
        )

    def lon_copy(i, c, side):
        return pltpu.make_async_remote_copy(
            src_ref=lon_send.at[i, c, side],
            dst_ref=lon_recv.at[i, c, 1 - side],
            send_sem=lon_ss.at[i, c, side],
            recv_sem=lon_rs.at[i, c, 1 - side],
            device_id={"lon": east if side else west},
            device_id_type=MESH,
        )

    def mix(i, c):
        columns = [jnp.zeros((lev, lanes), F32), jnp.zeros((lev, lanes), F32)]
        order = [0, lat_rows - 1] + list(range(1, lat_rows - 1))
        cs = slice(c * wide, (c + 1) * wide)
        for y in order:
            entrain = profs[0, pl.ds(y, lev, stride=lat_rows), :]
            detrain = profs[1, pl.ds(y, lev, stride=lat_rows), :]
            before = state[y, :, cs]
            lowered = (jnp.concatenate([detrain] * each, axis=1) * before).astype(BF16)
            mixing = jnp.dot(turned, lowered, preferred_element_type=F32)
            after = before + jnp.concatenate([entrain] * each, axis=1) * mixing
            mixed[y, :, cs] = after
            if y == 0:
                lat_send[i, c, 0] = after.astype(BF16)

                @pl.when(lat > 0)
                def _():
                    lat_copy(i, c, 0).start()

            if y == lat_rows - 1:
                lat_send[i, c, 1] = after.astype(BF16)

                @pl.when(lat < nlat - 1)
                def _():
                    lat_copy(i, c, 1).start()

            for t in range(each):
                at = y * each + t
                tile = after[:, t * lanes : (t + 1) * lanes]
                west_edge = tile if at == 0 else pltpu.roll(tile, at, 1)
                columns[0] = jnp.where(lane == at, west_edge, columns[0])
                columns[1] = jnp.where(lane == at, pltpu.roll(tile, at + 1, 1), columns[1])
        for side in range(2):
            lon_send[i, c, side] = columns[side].astype(BF16)
            lon_copy(i, c, side).start()

    def advance(i, c, y):
        for h in range(2):
            ks = slice(h * half, (h + 1) * half)
            f = [fracs[j, pl.ds(h * half * lat_rows + y, half, stride=lat_rows), :] for j in range(4)]
            remain = 1.0 - f[0] - f[1] - f[2] - f[3]
            from_west = lon_recv[i, c, 0].astype(F32)[ks]
            from_east = lon_recv[i, c, 1].astype(F32)[ks]
            for t in range(each):
                ts = slice(c * wide + t * lanes, c * wide + (t + 1) * lanes)
                own = slice(t * lanes, (t + 1) * lanes)
                at = y * each + t
                here = mixed[y, ks, ts]
                side_e = jnp.where(
                    lane_half == lanes - 1,
                    jnp.broadcast_to(from_east[:, at : at + 1], (half, lanes)),
                    pltpu.roll(here, lanes - 1, 1),
                )
                side_w = jnp.where(
                    lane_half == 0,
                    jnp.broadcast_to(from_west[:, at : at + 1], (half, lanes)),
                    pltpu.roll(here, 1, 1),
                )
                if y == lat_rows - 1:
                    north = lat_recv[i, c, 1, :, own].astype(F32)[ks]
                else:
                    north = mixed[y + 1, ks, ts]
                if y == 0:
                    south = lat_recv[i, c, 0, :, own].astype(F32)[ks]
                else:
                    south = mixed[y - 1, ks, ts]
                state[y, ks, ts] = remain * here + f[0] * side_e + f[1] * side_w + f[2] * north + f[3] * south

    def land(i, c):
        lon_copy(i, c, 0).wait_recv()
        lon_copy(i, c, 1).wait_recv()
        for y in range(1, lat_rows - 1):
            advance(i, c, y)

        @pl.when(lat < nlat - 1)
        def _():
            lat_copy(i, c, 0).wait_recv()

        @pl.when(lat > 0)
        def _():
            lat_copy(i, c, 1).wait_recv()

        advance(i, c, 0)
        advance(i, c, lat_rows - 1)

    width = levels + tracers + 2
    spare = lanes - width
    size = CAPACITY * SLOTS
    lane8 = lax.broadcasted_iota(jnp.int32, (SLOTS, lanes), 1)
    lane16 = lax.broadcasted_iota(jnp.int32, (16, lanes), 1).astype(F32)

    def force(g):
        for p in range(group):
            block = got[g * group + p].astype(F32)
            quarter = [block[q * SLOTS : (q + 1) * SLOTS] for q in range(4)]
            for q in range(4):
                slots[p * size + q * SLOTS : p * size + (q + 1) * SLOTS, :] = quarter[q]
            for q in range(2):
                low = pltpu.roll(quarter[2 * q], lanes - width, 1)
                high = pltpu.roll(quarter[2 * q + 1], lanes - width + spare, 1)
                at = p * size + (4 + q) * SLOTS
                slots[at : at + SLOTS, :] = jnp.where(lane8 < spare, low, high)
        for c in range(group * size // lanes):
            flipped = slots[c * lanes : (c + 1) * lanes, :].T
            weights = flipped[0:lev, :]
            row = flipped[levels + tracers : levels + tracers + 1, :]
            for y in range(lat_rows):
                lhs[y * lev : (y + 1) * lev, c * lanes : (c + 1) * lanes] = jnp.where(row == y, weights, 0.0).astype(BF16)
        for q in range(group * size // 16):
            here = slots[q * 16 : (q + 1) * 16, :]
            col = jnp.broadcast_to(here[:, width - 1 : width], (16, lanes)) == lane16
            for t in range(tracers):
                value = jnp.broadcast_to(here[:, levels + t : levels + t + 1], (16, lanes))
                rhs[q * 16 : (q + 1) * 16, t * lanes : (t + 1) * lanes] = jnp.where(col, value, 0.0).astype(BF16)
        acc[...] += jnp.dot(lhs[...], rhs[...], preferred_element_type=F32)

    def fill(g):
        @pl.loop(0, group)
        def _(p):
            @pl.when(g * group + p > 0)
            def _():
                all_copy(g * group + p).wait_recv()

        force(g)

    groups = devices // group
    per_wait = groups // (2 * CHAINS)

    mix(0, 0)
    send_all()
    for c in range(1, CHAINS):
        mix(0, c)

    def step(i, _):
        n = STEPS - 1 - i
        for f in range(4):
            at = pl.multiple_of((n * 4 + f) * rows, 8)
            fracs[f, 0:rows, :] = frac_ref[pl.ds(at, rows), :].astype(F32)
        for c in range(CHAINS):
            cs = slice(c * wide, (c + 1) * wide)

            @pl.when(i >= STEPS - 2)
            def _():
                for q in range(per_wait):
                    fill(((i - (STEPS - 2)) * CHAINS + c) * per_wait + q)

            land(i, c)

            @pl.when(i < STEPS - 1)
            def _():
                for y in range(lat_rows):
                    surf_ref[y, :, cs] += state[y, 0:8, cs]
                mix(i + 1, c)

        return 0

    lax.fori_loop(0, STEPS, step, 0)
    brows = tracers * lat_rows
    for y in range(lat_rows):
        for t in range(tracers):
            ts = slice(t * lanes, (t + 1) * lanes)
            at = y * tracers + t
            last = state[y, 0:1, ts] + acc[y * lev : y * lev + 1, ts]
            flat[at : at + 1, :] = surf_ref[y, 0:1, ts] + last
    low_ref[...] = flat[...].astype(BF16)

    def band_copy(d):
        return pltpu.make_async_remote_copy(
            src_ref=low_ref, dst_ref=lon_got.at[d], send_sem=ss_lon.at[d], recv_sem=rs_lon.at[d],
            device_id={"lon": lax.rem(lon + d, nlon)}, device_id_type=MESH,
        )

    def cross_copy(d):
        return pltpu.make_async_remote_copy(
            src_ref=own_ref, dst_ref=lat_got.at[d], send_sem=ss_lat.at[d], recv_sem=rs_lat.at[d],
            device_id={"lat": lax.rem(lat + d, nlat)}, device_id_type=MESH,
        )

    for d in range(1, nlon):
        band_copy(d).start()

    for y in range(lat_rows):
        for t in range(tracers):
            ts = slice(t * lanes, (t + 1) * lanes)
            full = state[y, :, ts] + acc[y * lev : (y + 1) * lev, ts]
            out_ref[pl.ds(t * rows + y, levels, stride=lat_rows), :] = full[0:levels]

    nrow = latm_ref.shape[0]
    pick = lax.broadcasted_iota(jnp.int32, (brows, nrow), 1) == lat * lat_rows + lax.broadcasted_iota(
        jnp.int32, (brows, nrow), 0
    ) % lat_rows
    own_rows = jnp.dot(jnp.where(pick, 1.0, 0.0).astype(BF16), latm_ref[...], preferred_element_type=F32).astype(BF16)
    spread = lax.broadcasted_iota(jnp.int32, (nrow, nrow * tracers), 0) == lax.broadcasted_iota(
        jnp.int32, (nrow, nrow * tracers), 1
    ) // tracers
    wide = jnp.dot(own_rows, jnp.where(spread, 1.0, 0.0).astype(BF16), preferred_element_type=F32)
    same = lax.broadcasted_iota(jnp.int32, (brows, nrow * tracers), 0) // lat_rows == lax.broadcasted_iota(
        jnp.int32, (brows, nrow * tracers), 1
    ) % tracers
    wide = jnp.where(same, wide, 0.0)

    contract = (((1,), (1,)), ((), ()))

    def part(d, block):
        source = lax.rem(lon - d + nlon, nlon)
        matrix = lonm_ref[:, pl.ds(pl.multiple_of(source * lanes, lanes), lanes)]
        return lax.dot_general(block, matrix, contract, preferred_element_type=F32)

    total = part(0, low_ref[...])
    for d in range(1, nlon):
        band_copy(d).wait_recv()
        total += part(d, lon_got[d])
    own_ref[...] = total.astype(BF16)
    for d in range(1, nlat):
        cross_copy(d).start()
    lat_got[0] = own_ref[...]
    blocks = []
    for d in range(nlat):
        if d:
            cross_copy(d).wait_recv()
        blocks.append(lat_got[d])
    gathered = jnp.concatenate(blocks, axis=0)
    turned = pltpu.roll(wide, (nlat - 1 - lat) * brows, 1)
    reordered = jnp.concatenate(
        [turned[:, (nlat - 1 - d) * brows : (nlat - d) * brows] for d in range(nlat)], axis=1
    ).astype(BF16)
    smoothed = jnp.dot(reordered, gathered, preferred_element_type=F32)
    smooth_ref[...] = smoothed.reshape(smooth_ref.shape)
    for d in range(1, nlon):
        band_copy(d).wait_send()
    for d in range(1, nlat):
        cross_copy(d).wait_send()
    for i in range(STEPS):
        for c in range(CHAINS):
            for side in range(2):
                lon_copy(i, c, side).wait_send()

            @pl.when(lat > 0)
            def _():
                lat_copy(i, c, 0).wait_send()

            @pl.when(lat < nlat - 1)
            def _():
                lat_copy(i, c, 1).wait_send()

    @pl.loop(1, devices)
    def _(d):
        all_copy(d).wait_send()


def shards(
    adjoint_in, fractions, profiles, kernel, obs_weights, obs_resid, obs_cols, obs_owner, obs_count, lat_matrix, lon_matrix
):
    tracers, levels, lat_rows, lanes = adjoint_in.shape
    lev = padded(levels)
    nlat, nlon = lax.axis_size("lat"), lax.axis_size("lon")
    devices = nlat * nlon
    blocks = obs_count.shape[0]
    nslots = blocks * SLOTS
    big = dict(vmem_limit_bytes=60 << 20)

    packed = pl.pallas_call(
        functools.partial(pack_kernel, levels, tracers, devices),
        out_shape=jax.ShapeDtypeStruct((devices, 4 * SLOTS, lanes), BF16),
        in_specs=[VMEM, VMEM, VMEM, SMEM, SMEM],
        out_specs=VMEM,
        scratch_shapes=[
            pltpu.VMEM((lanes, nslots), F32),
            pltpu.VMEM((devices * CAPACITY * SLOTS, lanes), F32),
            pltpu.SMEM((devices,), jnp.int32),
        ],
        compiler_params=pltpu.CompilerParams(**big),
        name="pack",
    )(obs_weights, obs_resid, obs_cols.reshape(1, nslots), obs_owner.reshape(blocks), obs_count)
    rows = levels * lat_rows
    group = min(16, devices)
    each = tracers // CHAINS
    size = CAPACITY * SLOTS
    adjoint, smoothed = pl.pallas_call(
        functools.partial(exchange_kernel, tracers, levels, lat_rows, group),
        out_shape=(
            jax.ShapeDtypeStruct((tracers * rows, lanes), F32),
            jax.ShapeDtypeStruct((tracers, lat_rows, lanes), F32),
        ),
        in_specs=[VMEM] * 7,
        out_specs=(VMEM, VMEM),
        scratch_shapes=[
            pltpu.VMEM((lat_rows, lev, tracers * lanes), F32),
            pltpu.VMEM((lat_rows, 8, tracers * lanes), F32),
            pltpu.VMEM((lat_rows, lev, tracers * lanes), F32),
            pltpu.VMEM((4, lev * lat_rows, lanes), F32),
            pltpu.VMEM((2, lev * lat_rows, lanes), F32),
            pltpu.VMEM((lanes, lanes), F32),
            pltpu.VMEM((STEPS, CHAINS, 2, lev, each * lanes), BF16),
            pltpu.VMEM((STEPS, CHAINS, 2, lev, each * lanes), BF16),
            pltpu.VMEM((STEPS, CHAINS, 2, lev, lanes), BF16),
            pltpu.VMEM((STEPS, CHAINS, 2, lev, lanes), BF16),
            pltpu.SemaphoreType.DMA((STEPS, CHAINS, 2)),
            pltpu.SemaphoreType.DMA((STEPS, CHAINS, 2)),
            pltpu.SemaphoreType.DMA((STEPS, CHAINS, 2)),
            pltpu.SemaphoreType.DMA((STEPS, CHAINS, 2)),
            pltpu.VMEM((devices, 4 * SLOTS, lanes), BF16),
            pltpu.VMEM((lat_rows * lev, tracers * lanes), F32),
            pltpu.VMEM((group * size, lanes), F32),
            pltpu.VMEM((lat_rows * lev, group * size), BF16),
            pltpu.VMEM((group * size, tracers * lanes), BF16),
            pltpu.VMEM((lat_rows * tracers, lanes), F32),
            pltpu.VMEM((lat_rows * tracers, lanes), BF16),
            pltpu.VMEM((lat_rows * tracers, lanes), BF16),
            pltpu.VMEM((nlon, lat_rows * tracers, lanes), BF16),
            pltpu.VMEM((nlat, lat_rows * tracers, lanes), BF16),
            pltpu.SemaphoreType.DMA((devices,)),
            pltpu.SemaphoreType.DMA((devices,)),
            pltpu.SemaphoreType.DMA((nlon,)),
            pltpu.SemaphoreType.DMA((nlon,)),
            pltpu.SemaphoreType.DMA((nlat,)),
            pltpu.SemaphoreType.DMA((nlat,)),
        ],
        compiler_params=pltpu.CompilerParams(collective_id=0, has_side_effects=True, **big),
        name="exchange",
    )(
        adjoint_in.reshape(tracers * rows, lanes),
        fractions.reshape(STEPS * 4 * rows, lanes),
        profiles.reshape(2 * rows, lanes),
        kernel,
        packed,
        lon_matrix,
        lat_matrix,
    )
    return adjoint.reshape(adjoint_in.shape), smoothed


def solution(mesh):
    placed = (
        P(None, None, "lat", "lon"),
        P(None, None, None, "lat", "lon"),
        P(None, None, "lat", "lon"),
        P(),
        P(None, ("lat", "lon")),
        P(None, ("lat", "lon")),
        P(("lat", "lon")),
        P(("lat", "lon"), None),
        P(("lat", "lon")),
        P(),
        P("lon", None),
    )
    return jax.shard_map(
        shards,
        mesh=mesh,
        in_specs=placed,
        out_specs=(P(None, None, "lat", "lon"), P(None, "lat", "lon")),
        check_vma=False,
    )
```

time: 95.8 us -> 81 us (0.85)
  starting transfers between devices: 11.5 us -> 0 us
  Pallas kernels: 81.1 us -> 77.1 us
    all_to_all x1 -> x0, starting transfers between devices: 11.5 us -> none  [shards(): received = lax.all_to_all(packed, ('lat', 'lon'), 0, 0, tiled=True)]
    pallas_call x3 -> x1, Pallas kernels: 72 us -> 68.1 us  [shards(): pl.pallas_call(functools.partial(exchange_kernel, tracers, levels, lat_ro...]
    unnamed x3 -> x4, local copies, waits for them, and re-layouts: 2.3 us -> 3.06 us
  transfers between devices with their start and end apart: 1 -> 0, of which waited for: 0 -> 0; matrix products, arithmetic and copies ran while one was open for 0% -> 0% of each run, Pallas kernels for 42% -> 0%
where the time goes in v1:
time: 81 us; the launch traced here: 80.8 us
  Pallas kernels  77.1 us (95%)
  local copies, waits for them, and re-layouts  3.06 us (4%)
    pallas_call x1, Pallas kernels, shards(): pl.pallas_call(functools.partial(exchange_kernel, tracers, levels, lat_ro...  68.1 us
    pallas_call x1, Pallas kernels, shards(): pl.pallas_call(functools.partial(pack_kernel, levels, tracers, devices),...  9.02 us
    unnamed x4, local copies, waits for them, and re-layouts  3.06 us

profile of v1, /device:TPU:1, one launch (start us, length us, event | category | flops | bytes accessed | tf_op | source)
XLA Modules:
  0.0 80.8 jit_solution(18376638264567753697)
XLA Ops:
  0.6 9.0 %pack.1.packed_ref = bf16[128,32,128]{2,1,0:T(8,128)(2,1)} custom-call(bf16[79,4096]{1,0:T(8,128)(2,1)} %w_ref.1, bf16[4,4096]{1,0:T(4,128)(2,1)} %r_ref.1, s32[1,4096]{1,0:T(1,128)} %bitcast.10, s32[512]{0:T(512)} %bitcast.11, s32[512]{0:T(512)} %count_ref.1), custom_call_target="tpu_custom_call" | custom-call | tf_op jit(solution)/shard_map/pack/pallas_call | solution.py:430
  9.7 68.1 %exchange.1 = (f32[2528,128]{1,0:T(8,128)}, f32[4,8,128]{2,1,0:T(8,128)}) custom-call(f32[2528,128]{1,0:T(8,128)} %bitcast.8, bf16[10112,128]{1,0:T(8,128)(2,1)} %bitcast.6, bf16[1264,128]{1,0:T(8,128)(2,1)} %bitcast.9, bf16[79,79]{1,0:T(8,128)(2,1)} %ker_ref.1, bf16[128,32,128]{2,1,0:T(8,128)(2,1)} %pack.1.packed_ref, bf16[128,2048]{1,0:T(8,128)(2,1)} %lonm_ref.1, ...), custom_call_target="tpu_custom_call" | custom-call | tf_op jit(solution)/shard_map/exchange/pallas_call | solution.py:447
  77.7 0.0 copy-start
  77.7 2.4 %copy.15 = f32[4,79,8,128]{3,2,1,0:T(8,128)} copy(f32[4,79,8,128]{3,2,1,0:T(8,128)} %bitcast.7) | data formatting | bytes 2588672
  80.2 0.0 copy-done
  80.2 0.6 copy.16
Async XLA Ops:
  77.7 2.5 %copy-start = (f32[4,8,128]{2,1,0:T(8,128)S(1)}, f32[4,8,128]{2,1,0:T(8,128)}, u32[]{:S(2)}) copy-start(f32[4,8,128]{2,1,0:T(8,128)} %get-tuple-element.9) | copy-start | bytes 49156

commit v2 on v1

--- a/solution.py
+++ b/solution.py
@@ -11,7 +11,11 @@
 CAPACITY = 6
 SLOTS = 8
 CHAINS = 2
+SEND_NUM = 2
+USE_FROM = 1
+USE_NUM, USE_DEN = 4, 3
 MESH = pl.DeviceIdType.MESH
+LOGICAL = pl.DeviceIdType.LOGICAL
 F32 = jnp.float32
 BF16 = jnp.bfloat16
 VMEM = pl.BlockSpec(memory_space=pltpu.VMEM)
@@ -22,59 +26,14 @@
     return -(-levels // 16) * 16
 
 
-def pack_kernel(levels, tracers, devices, w_ref, r_ref, c_ref, owner_ref, count_ref, out_ref, feat, rows, seen):
-    blocks = owner_ref.shape[0]
-    lanes = 128
-    per_chunk = lanes // SLOTS
-    feat[0:levels, :] = w_ref[...].astype(F32)
-    feat[levels : levels + tracers, :] = r_ref[...].astype(F32)
-    cell = c_ref[...]
-    feat[levels + tracers : levels + tracers + 1, :] = (cell // lanes).astype(F32)
-    feat[levels + tracers + 1 : levels + tracers + 2, :] = (cell % lanes).astype(F32)
-    rows[...] = jnp.zeros_like(rows)
-
-    @pl.loop(0, devices)
-    def _(d):
-        seen[d] = 0
-
-    slot = lax.broadcasted_iota(jnp.int32, (SLOTS, lanes), 0)
-
-    @pl.loop(0, blocks // per_chunk)
-    def _(chunk):
-        at = pl.multiple_of(chunk * lanes, lanes)
-        turned = feat[:, pl.ds(at, lanes)].T
-        for i in range(per_chunk):
-            b = chunk * per_chunk + i
-            owner = owner_ref[b]
-            rank = seen[owner]
-            seen[owner] = rank + 1
-            place = pl.multiple_of((owner * CAPACITY + rank) * SLOTS, SLOTS)
-            block = turned[i * SLOTS : (i + 1) * SLOTS, :]
-            rows[pl.ds(place, SLOTS), :] = jnp.where(slot < count_ref[b], block, 0.0)
-
-    width = levels + tracers + 2
-    spare = lanes - width
-    lane = lax.broadcasted_iota(jnp.int32, (SLOTS, lanes), 1)
-
-    @pl.loop(0, devices, unroll=4)
-    def _(d):
-        base = d * (CAPACITY * SLOTS)
-        got = [rows[pl.ds(pl.multiple_of(base + i * SLOTS, SLOTS), SLOTS), :] for i in range(CAPACITY)]
-        pieces = []
-        for i in range(4):
-            extra = got[4 + i // 2]
-            shift = width if i % 2 == 0 else width - spare
-            pieces.append(jnp.where(lane < width, got[i], pltpu.roll(extra, shift, 1)))
-        out_ref[d] = jnp.concatenate(pieces, axis=0).astype(BF16)
-
-
 def exchange_kernel(
     tracers, levels, lat_rows, group,
-    adj_ref, frac_ref, prof_ref, ker_ref, packed_ref, lonm_ref, latm_ref,
+    adj_ref, frac_ref, prof_ref, ker_ref, w_ref, r_ref, cell_ref, owner_ref, count_ref, lonm_ref, latm_ref,
     out_ref, smooth_ref,
     state, surf_ref, mixed, fracs, profs, square,
     lat_send, lat_recv, lon_send, lon_recv,
     lat_ss, lat_rs, lon_ss, lon_rs,
+    feat, block_rows, table_v, table, table_sem, packed_ref,
     got, acc, slots, lhs, rhs, flat, low_ref, own_ref, lon_got, lat_got,
     all_ss, all_rs, ss_lon, rs_lon, ss_lat, rs_lat,
 ):
@@ -90,12 +49,12 @@
     barrier = pltpu.get_barrier_semaphore()
 
     def place(d):
-        to = lax.rem(me + d, devices)
-        return to, {"lat": to // nlon, "lon": lax.rem(to, nlon)}
+        to = me + d
+        return jnp.where(to < devices, to, to - devices)
 
     @pl.loop(1, devices)
     def _(d):
-        pl.semaphore_signal(barrier, inc=1, device_id=place(d)[1], device_id_type=MESH)
+        pl.semaphore_signal(barrier, inc=1, device_id=place(d), device_id_type=LOGICAL)
 
     @pl.when(lat == 0)
     def _():
@@ -124,21 +83,96 @@
             state[y, 0:levels, t * lanes : (t + 1) * lanes] = adj_ref[pl.ds(t * rows + y, levels, stride=lat_rows), :]
     surf_ref[...] = jnp.zeros_like(surf_ref)
     acc[...] = jnp.zeros_like(acc)
+
+    blocks = owner_ref.shape[1]
+    owner_row = owner_ref[...]
+    parts = [owner_row[:, j * lanes : (j + 1) * lanes] for j in range(blocks // lanes)]
+    owner_col = jnp.concatenate([jnp.broadcast_to(p, (lanes, lanes)).T for p in parts], axis=0)
+    number = lax.broadcasted_iota(jnp.int32, (blocks, lanes), 0)
+    across = lax.broadcasted_iota(jnp.int32, (blocks, lanes), 1)
+    earlier = jnp.zeros((blocks, lanes), jnp.int32)
+    for j, p in enumerate(parts):
+        earlier += jnp.where((owner_col == p) & (across + j * lanes < number), 1, 0)
+    rank = jnp.sum(earlier, axis=1, keepdims=True)
+    mine = jnp.where(owner_col == across, jnp.broadcast_to(rank, (blocks, lanes)), CAPACITY)
+    behind = number - blocks
+    for k in range(CAPACITY):
+        found = jnp.sum(jnp.where(mine == k, behind, 0), axis=0, keepdims=True) + blocks
+        table_v[k : k + 1, :] = found
+    table_v[CAPACITY:8, :] = jnp.zeros((8 - CAPACITY, lanes), jnp.int32)
+    to_scalar = pltpu.make_async_copy(table_v, table, table_sem)
+    to_scalar.start()
+
+    width = levels + tracers + 2
+    spare = lanes - width
+    nslots = blocks * SLOTS
+    feat[levels // 8 * 8 :, :] = jnp.zeros((lanes - levels // 8 * 8, nslots), F32)
+    feat[0:levels, :] = w_ref[...].astype(F32)
+    feat[levels : levels + tracers, :] = r_ref[...].astype(F32)
+    cell = cell_ref[...]
+    feat[width - 2 : width - 1, :] = lax.shift_right_logical(cell, 7).astype(F32)
+    feat[width - 1 : width, :] = (cell & (lanes - 1)).astype(F32)
+    block_rows[blocks] = jnp.zeros((SLOTS, lanes), F32)
+    per_tile = lanes // SLOTS
+
+    @pl.loop(0, nslots // lanes, unroll=2)
+    def _(c):
+        at = pl.multiple_of(c * lanes, lanes)
+        block_rows[pl.ds(c * per_tile, per_tile)] = feat[:, pl.ds(at, lanes)].T.reshape(per_tile, SLOTS, lanes)
+
+    to_scalar.wait()
+    slot_of = lax.broadcasted_iota(jnp.int32, (SLOTS, lanes), 0)
+    lane8 = lax.broadcasted_iota(jnp.int32, (SLOTS, lanes), 1)
+
+    def pack(to):
+        six = []
+        for k in range(CAPACITY):
+            b = table[k, to]
+            six.append(jnp.where(slot_of < count_ref[b], block_rows[b], 0.0))
+        pieces = []
+        for q in range(4):
+            extra = pltpu.roll(six[4 + q // 2], width if q % 2 == 0 else width - spare, 1)
+            pieces.append(jnp.where(lane8 < width, six[q], extra))
+        return jnp.concatenate(pieces, axis=0).astype(BF16)
+
     pl.semaphore_wait(barrier, devices - 1)
 
     def all_copy(d):
-        to, where = place(d)
+        to = place(d)
         return pltpu.make_async_remote_copy(
-            src_ref=packed_ref.at[to], dst_ref=got.at[d], send_sem=all_ss.at[d], recv_sem=all_rs.at[d],
-            device_id=where, device_id_type=MESH,
+            src_ref=packed_ref.at[to], dst_ref=got.at[d - 1], send_sem=all_ss, recv_sem=all_rs.at[(d - 1) // group],
+            device_id=to, device_id_type=LOGICAL,
         )
 
-    def send_all():
-        @pl.loop(1, devices)
+    def all_wait(g, count):
+        part = got.at[pl.ds(g * group, count)]
+        return pltpu.make_async_remote_copy(
+            src_ref=part, dst_ref=part, send_sem=all_ss, recv_sem=all_rs.at[g], device_id=me, device_id_type=LOGICAL
+        )
+
+    groups = devices // group
+
+    def send_some(slot):
+        @pl.loop(sent(slot) * group, sent(slot + 1) * group)
         def _(d):
-            all_copy(d).start()
-
-    got[0] = packed_ref[me]
+            @pl.when(d < devices - 1)
+            def _():
+                to = place(d + 1)
+                packed_ref[to] = pack(to)
+
+        @pl.loop(sent(slot) * group, sent(slot + 1) * group)
+        def _(d):
+            @pl.when(d < devices - 1)
+            def _():
+                all_copy(d + 1).start()
+
+    def sent(slot):
+        return jnp.minimum(groups, slot * SEND_NUM)
+
+    def used(slot):
+        return jnp.minimum(groups, jnp.maximum(0, (slot - USE_FROM) * USE_NUM // USE_DEN))
+
+    got[devices - 1] = pack(me)
 
     lane = lax.broadcasted_iota(jnp.int32, (lev, lanes), 1)
     half = lev // 2
@@ -251,10 +285,7 @@
         advance(i, c, 0)
         advance(i, c, lat_rows - 1)
 
-    width = levels + tracers + 2
-    spare = lanes - width
     size = CAPACITY * SLOTS
-    lane8 = lax.broadcasted_iota(jnp.int32, (SLOTS, lanes), 1)
     lane16 = lax.broadcasted_iota(jnp.int32, (16, lanes), 1).astype(F32)
 
     def force(g):
@@ -283,21 +314,19 @@
         acc[...] += jnp.dot(lhs[...], rhs[...], preferred_element_type=F32)
 
     def fill(g):
-        @pl.loop(0, group)
-        def _(p):
-            @pl.when(g * group + p > 0)
-            def _():
-                all_copy(g * group + p).wait_recv()
+        @pl.when(g < groups - 1)
+        def _():
+            all_wait(g, group).wait_recv()
+
+        @pl.when(g == groups - 1)
+        def _():
+            all_wait(g, group - 1).wait_recv()
 
         force(g)
 
-    groups = devices // group
-    per_wait = groups // (2 * CHAINS)
-
-    mix(0, 0)
-    send_all()
-    for c in range(1, CHAINS):
+    for c in range(CHAINS):
         mix(0, c)
+        send_some(c)
 
     def step(i, _):
         n = STEPS - 1 - i
@@ -307,11 +336,8 @@
         for c in range(CHAINS):
             cs = slice(c * wide, (c + 1) * wide)
 
-            @pl.when(i >= STEPS - 2)
-            def _():
-                for q in range(per_wait):
-                    fill(((i - (STEPS - 2)) * CHAINS + c) * per_wait + q)
-
+            slot = i * CHAINS + c
+            pl.loop(used(slot - 1), used(slot))(fill)
             land(i, c)
 
             @pl.when(i < STEPS - 1)
@@ -319,6 +345,7 @@
                 for y in range(lat_rows):
                     surf_ref[y, :, cs] += state[y, 0:8, cs]
                 mix(i + 1, c)
+                send_some((i + 1) * CHAINS + c)
 
         return 0
 
@@ -411,9 +438,10 @@
             def _():
                 lat_copy(i, c, 1).wait_send()
 
-    @pl.loop(1, devices)
-    def _(d):
-        all_copy(d).wait_send()
+    sent_all = packed_ref.at[pl.ds(0, devices - 1)]
+    pltpu.make_async_remote_copy(
+        src_ref=sent_all, dst_ref=sent_all, send_sem=all_ss, recv_sem=all_rs.at[0], device_id=me, device_id_type=LOGICAL
+    ).wait_send()
 
 
 def shards(
@@ -427,19 +455,6 @@
     nslots = blocks * SLOTS
     big = dict(vmem_limit_bytes=60 << 20)
 
-    packed = pl.pallas_call(
-        functools.partial(pack_kernel, levels, tracers, devices),
-        out_shape=jax.ShapeDtypeStruct((devices, 4 * SLOTS, lanes), BF16),
-        in_specs=[VMEM, VMEM, VMEM, SMEM, SMEM],
-        out_specs=VMEM,
-        scratch_shapes=[
-            pltpu.VMEM((lanes, nslots), F32),
-            pltpu.VMEM((devices * CAPACITY * SLOTS, lanes), F32),
-            pltpu.SMEM((devices,), jnp.int32),
-        ],
-        compiler_params=pltpu.CompilerParams(**big),
-        name="pack",
-    )(obs_weights, obs_resid, obs_cols.reshape(1, nslots), obs_owner.reshape(blocks), obs_count)
     rows = levels * lat_rows
     group = min(16, devices)
     each = tracers // CHAINS
@@ -450,7 +465,7 @@
             jax.ShapeDtypeStruct((tracers * rows, lanes), F32),
             jax.ShapeDtypeStruct((tracers, lat_rows, lanes), F32),
         ),
-        in_specs=[VMEM] * 7,
+        in_specs=[VMEM] * 8 + [SMEM] + [VMEM] * 2,
         out_specs=(VMEM, VMEM),
         scratch_shapes=[
             pltpu.VMEM((lat_rows, lev, tracers * lanes), F32),
@@ -467,6 +482,12 @@
             pltpu.SemaphoreType.DMA((STEPS, CHAINS, 2)),
             pltpu.SemaphoreType.DMA((STEPS, CHAINS, 2)),
             pltpu.SemaphoreType.DMA((STEPS, CHAINS, 2)),
+            pltpu.VMEM((lanes, nslots), F32),
+            pltpu.VMEM((blocks + 1, SLOTS, lanes), F32),
+            pltpu.VMEM((8, lanes), jnp.int32),
+            pltpu.SMEM((8, lanes), jnp.int32),
+            pltpu.SemaphoreType.DMA,
+            pltpu.VMEM((devices, 4 * SLOTS, lanes), BF16),
             pltpu.VMEM((devices, 4 * SLOTS, lanes), BF16),
             pltpu.VMEM((lat_rows * lev, tracers * lanes), F32),
             pltpu.VMEM((group * size, lanes), F32),
@@ -477,8 +498,8 @@
             pltpu.VMEM((lat_rows * tracers, lanes), BF16),
             pltpu.VMEM((nlon, lat_rows * tracers, lanes), BF16),
             pltpu.VMEM((nlat, lat_rows * tracers, lanes), BF16),
-            pltpu.SemaphoreType.DMA((devices,)),
-            pltpu.SemaphoreType.DMA((devices,)),
+            pltpu.SemaphoreType.DMA,
+            pltpu.SemaphoreType.DMA((devices // group,)),
             pltpu.SemaphoreType.DMA((nlon,)),
             pltpu.SemaphoreType.DMA((nlon,)),
             pltpu.SemaphoreType.DMA((nlat,)),
@@ -491,7 +512,11 @@
         fractions.reshape(STEPS * 4 * rows, lanes),
         profiles.reshape(2 * rows, lanes),
         kernel,
-        packed,
+        obs_weights,
+        obs_resid,
+        obs_cols.reshape(1, nslots),
+        obs_owner.reshape(1, blocks),
+        jnp.pad(obs_count, (0, lanes)),
         lon_matrix,
         lat_matrix,
     )

time: 81 us -> 65.7 us (0.81)
  Pallas kernels: 77.1 us -> 60.6 us
  local copies, waits for them, and re-layouts: 3.06 us -> 4.34 us
    pallas_call x1 -> x0, Pallas kernels: 9.02 us -> none  [shards(): pl.pallas_call(functools.partial(pack_kernel, levels, tracers, devices),...]
    pallas_call x1, Pallas kernels: 68.1 us -> 60.6 us  [shards(): pl.pallas_call(functools.partial(exchange_kernel, tracers, levels, lat_ro...]
    pad x0 -> x1, local copies, waits for them, and re-layouts: none -> 1.28 us  [shards(): jnp.pad(obs_count, (0, lanes))]
where the time goes in v2:
time: 65.7 us; the launch traced here: 65.6 us
  Pallas kernels  60.6 us (92%)
  local copies, waits for them, and re-layouts  4.34 us (7%)
    pallas_call x1, Pallas kernels, shards(): pl.pallas_call(functools.partial(exchange_kernel, tracers, levels, lat_ro...  60.6 us
    unnamed x4, local copies, waits for them, and re-layouts  3.06 us

profile of v2, /device:TPU:1, one launch (start us, length us, event | category | flops | bytes accessed | tf_op | source)
XLA Modules:
  0.0 65.6 jit_solution(7256589096944526829)
XLA Ops:
  0.6 1.3 %pad.4.count_ref = s32[640]{0:T(1024)} pad(s32[512]{0:T(512)} %param.19, s32[]{:T(128)} %constant.0.clone.1), padding=0_128 | pad | bytes 4612 | tf_op jit(solution)/shard_map/jit(_pad)/pad | solution.py:519
  1.9 60.6 %exchange.1 = (f32[2528,128]{1,0:T(8,128)}, f32[4,8,128]{2,1,0:T(8,128)}) custom-call(f32[2528,128]{1,0:T(8,128)} %bitcast.8, bf16[10112,128]{1,0:T(8,128)(2,1)} %bitcast.6, bf16[1264,128]{1,0:T(8,128)(2,1)} %bitcast.9, bf16[79,79]{1,0:T(8,128)(2,1)} %ker_ref.1, bf16[79,4096]{1,0:T(8,128)(2,1)} %w_ref.1, bf16[4,4096]{1,0:T(4,128)(2,1)} %r_ref.1, ...), custom_call_target="tpu_custom_call" | custom-call | tf_op jit(solution)/shard_map/exchange/pallas_call | solution.py:462
  62.5 0.0 copy-start
  62.5 2.4 %copy.15 = f32[4,79,8,128]{3,2,1,0:T(8,128)} copy(f32[4,79,8,128]{3,2,1,0:T(8,128)} %bitcast.7) | data formatting | bytes 2588672
  65.0 0.0 copy-done
  65.0 0.6 copy.16
Async XLA Ops:
  62.5 2.5 %copy-start = (f32[4,8,128]{2,1,0:T(8,128)S(1)}, f32[4,8,128]{2,1,0:T(8,128)}, u32[]{:S(2)}) copy-start(f32[4,8,128]{2,1,0:T(8,128)} %get-tuple-element.9) | copy-start | bytes 49156

commit v3 on v2

--- a/solution.py
+++ b/solution.py
@@ -12,8 +12,8 @@
 SLOTS = 8
 CHAINS = 2
 SEND_NUM = 2
-USE_FROM = 1
-USE_NUM, USE_DEN = 4, 3
+USE_FROM = 0
+USE_NUM, USE_DEN = 8, 7
 MESH = pl.DeviceIdType.MESH
 LOGICAL = pl.DeviceIdType.LOGICAL
 F32 = jnp.float32
@@ -34,7 +34,7 @@
     lat_send, lat_recv, lon_send, lon_recv,
     lat_ss, lat_rs, lon_ss, lon_rs,
     feat, block_rows, table_v, table, table_sem, packed_ref,
-    got, acc, slots, lhs, rhs, flat, low_ref, own_ref, lon_got, lat_got,
+    got, acc, slots, lhs, rhs, flat, low_ref, own_ref, lon_got, lat_got, lon_turned, lat_ordered,
     all_ss, all_rs, ss_lon, rs_lon, ss_lat, rs_lat,
 ):
     lanes = 128
@@ -95,11 +95,15 @@
         earlier += jnp.where((owner_col == p) & (across + j * lanes < number), 1, 0)
     rank = jnp.sum(earlier, axis=1, keepdims=True)
     mine = jnp.where(owner_col == across, jnp.broadcast_to(rank, (blocks, lanes)), CAPACITY)
-    behind = number - blocks
+    count_row = count_ref[...]
+    count_col = jnp.concatenate(
+        [jnp.broadcast_to(count_row[:, j * lanes : (j + 1) * lanes], (lanes, lanes)).T for j in range(blocks // lanes)], axis=0
+    )
+    table_v[...] = jnp.zeros_like(table_v)
     for k in range(CAPACITY):
-        found = jnp.sum(jnp.where(mine == k, behind, 0), axis=0, keepdims=True) + blocks
-        table_v[k : k + 1, :] = found
-    table_v[CAPACITY:8, :] = jnp.zeros((8 - CAPACITY, lanes), jnp.int32)
+        hit = mine == k
+        table_v[k : k + 1, :] = jnp.sum(jnp.where(hit, number, 0), axis=0, keepdims=True)
+        table_v[8 + k : 9 + k, :] = jnp.sum(jnp.where(hit, count_col, 0), axis=0, keepdims=True)
     to_scalar = pltpu.make_async_copy(table_v, table, table_sem)
     to_scalar.start()
 
@@ -112,7 +116,6 @@
     cell = cell_ref[...]
     feat[width - 2 : width - 1, :] = lax.shift_right_logical(cell, 7).astype(F32)
     feat[width - 1 : width, :] = (cell & (lanes - 1)).astype(F32)
-    block_rows[blocks] = jnp.zeros((SLOTS, lanes), F32)
     per_tile = lanes // SLOTS
 
     @pl.loop(0, nslots // lanes, unroll=2)
@@ -128,7 +131,7 @@
         six = []
         for k in range(CAPACITY):
             b = table[k, to]
-            six.append(jnp.where(slot_of < count_ref[b], block_rows[b], 0.0))
+            six.append(jnp.where(slot_of < table[8 + k, to], block_rows[b], 0.0))
         pieces = []
         for q in range(4):
             extra = pltpu.roll(six[4 + q // 2], width if q % 2 == 0 else width - spare, 1)
@@ -153,11 +156,11 @@
     groups = devices // group
 
     def send_some(slot):
-        @pl.loop(sent(slot) * group, sent(slot + 1) * group)
-        def _(d):
-            @pl.when(d < devices - 1)
-            def _():
-                to = place(d + 1)
+        @pl.loop(sent(slot), sent(slot + 1))
+        def _(g):
+            @pl.loop(0, group, unroll=8)
+            def _(p):
+                to = place(g * group + p + 1)
                 packed_ref[to] = pack(to)
 
         @pl.loop(sent(slot) * group, sent(slot + 1) * group)
@@ -328,6 +331,33 @@
         mix(0, c)
         send_some(c)
 
+    def matrices():
+        brows = tracers * lat_rows
+        nrow = latm_ref.shape[0]
+        pick = lax.broadcasted_iota(jnp.int32, (brows, nrow), 1) == lat * lat_rows + lax.broadcasted_iota(
+            jnp.int32, (brows, nrow), 0
+        ) % lat_rows
+        own_rows = jnp.dot(jnp.where(pick, 1.0, 0.0).astype(BF16), latm_ref[...], preferred_element_type=F32).astype(BF16)
+        spread = lax.broadcasted_iota(jnp.int32, (nrow, nrow * tracers), 0) == lax.broadcasted_iota(
+            jnp.int32, (nrow, nrow * tracers), 1
+        ) // tracers
+        wide = jnp.dot(own_rows, jnp.where(spread, 1.0, 0.0).astype(BF16), preferred_element_type=F32)
+        same = lax.broadcasted_iota(jnp.int32, (brows, nrow * tracers), 0) // lat_rows == lax.broadcasted_iota(
+            jnp.int32, (brows, nrow * tracers), 1
+        ) % tracers
+        wide = jnp.where(same, wide, 0.0)
+
+        rolled = pltpu.roll(wide, (nlat - 1 - lat) * brows, 1)
+        lat_ordered[...] = jnp.concatenate(
+            [rolled[:, (nlat - 1 - d) * brows : (nlat - d) * brows] for d in range(nlat)], axis=1
+        ).astype(BF16)
+
+        @pl.loop(0, nlon, unroll=2)
+        def _(d):
+            source = lax.rem(lon - d + nlon, nlon)
+            part = lonm_ref[:, pl.ds(pl.multiple_of(source * lanes, lanes), lanes)].astype(F32)
+            lon_turned[pl.ds(pl.multiple_of(d * lanes, lanes), lanes), :] = part.T.astype(BF16)
+
     def step(i, _):
         n = STEPS - 1 - i
         for f in range(4):
@@ -337,6 +367,8 @@
             cs = slice(c * wide, (c + 1) * wide)
 
             slot = i * CHAINS + c
+            if c == 0:
+                pl.when(i == 2)(matrices)
             pl.loop(used(slot - 1), used(slot))(fill)
             land(i, c)
 
@@ -380,32 +412,11 @@
             full = state[y, :, ts] + acc[y * lev : (y + 1) * lev, ts]
             out_ref[pl.ds(t * rows + y, levels, stride=lat_rows), :] = full[0:levels]
 
-    nrow = latm_ref.shape[0]
-    pick = lax.broadcasted_iota(jnp.int32, (brows, nrow), 1) == lat * lat_rows + lax.broadcasted_iota(
-        jnp.int32, (brows, nrow), 0
-    ) % lat_rows
-    own_rows = jnp.dot(jnp.where(pick, 1.0, 0.0).astype(BF16), latm_ref[...], preferred_element_type=F32).astype(BF16)
-    spread = lax.broadcasted_iota(jnp.int32, (nrow, nrow * tracers), 0) == lax.broadcasted_iota(
-        jnp.int32, (nrow, nrow * tracers), 1
-    ) // tracers
-    wide = jnp.dot(own_rows, jnp.where(spread, 1.0, 0.0).astype(BF16), preferred_element_type=F32)
-    same = lax.broadcasted_iota(jnp.int32, (brows, nrow * tracers), 0) // lat_rows == lax.broadcasted_iota(
-        jnp.int32, (brows, nrow * tracers), 1
-    ) % tracers
-    wide = jnp.where(same, wide, 0.0)
-
-    contract = (((1,), (1,)), ((), ()))
-
-    def part(d, block):
-        source = lax.rem(lon - d + nlon, nlon)
-        matrix = lonm_ref[:, pl.ds(pl.multiple_of(source * lanes, lanes), lanes)]
-        return lax.dot_general(block, matrix, contract, preferred_element_type=F32)
-
-    total = part(0, low_ref[...])
+    lon_got[0] = low_ref[...]
     for d in range(1, nlon):
         band_copy(d).wait_recv()
-        total += part(d, lon_got[d])
-    own_ref[...] = total.astype(BF16)
+    band = jnp.concatenate([lon_got[d] for d in range(nlon)], axis=1)
+    own_ref[...] = jnp.dot(band, lon_turned[...], preferred_element_type=F32).astype(BF16)
     for d in range(1, nlat):
         cross_copy(d).start()
     lat_got[0] = own_ref[...]
@@ -415,11 +426,7 @@
             cross_copy(d).wait_recv()
         blocks.append(lat_got[d])
     gathered = jnp.concatenate(blocks, axis=0)
-    turned = pltpu.roll(wide, (nlat - 1 - lat) * brows, 1)
-    reordered = jnp.concatenate(
-        [turned[:, (nlat - 1 - d) * brows : (nlat - d) * brows] for d in range(nlat)], axis=1
-    ).astype(BF16)
-    smoothed = jnp.dot(reordered, gathered, preferred_element_type=F32)
+    smoothed = jnp.dot(lat_ordered[...], gathered, preferred_element_type=F32)
     smooth_ref[...] = smoothed.reshape(smooth_ref.shape)
     for d in range(1, nlon):
         band_copy(d).wait_send()
@@ -465,7 +472,7 @@
             jax.ShapeDtypeStruct((tracers * rows, lanes), F32),
             jax.ShapeDtypeStruct((tracers, lat_rows, lanes), F32),
         ),
-        in_specs=[VMEM] * 8 + [SMEM] + [VMEM] * 2,
+        in_specs=[VMEM] * 11,
         out_specs=(VMEM, VMEM),
         scratch_shapes=[
             pltpu.VMEM((lat_rows, lev, tracers * lanes), F32),
@@ -483,9 +490,9 @@
             pltpu.SemaphoreType.DMA((STEPS, CHAINS, 2)),
             pltpu.SemaphoreType.DMA((STEPS, CHAINS, 2)),
             pltpu.VMEM((lanes, nslots), F32),
-            pltpu.VMEM((blocks + 1, SLOTS, lanes), F32),
-            pltpu.VMEM((8, lanes), jnp.int32),
-            pltpu.SMEM((8, lanes), jnp.int32),
+            pltpu.VMEM((blocks, SLOTS, lanes), F32),
+            pltpu.VMEM((16, lanes), jnp.int32),
+            pltpu.SMEM((16, lanes), jnp.int32),
             pltpu.SemaphoreType.DMA,
             pltpu.VMEM((devices, 4 * SLOTS, lanes), BF16),
             pltpu.VMEM((devices, 4 * SLOTS, lanes), BF16),
@@ -498,6 +505,8 @@
             pltpu.VMEM((lat_rows * tracers, lanes), BF16),
             pltpu.VMEM((nlon, lat_rows * tracers, lanes), BF16),
             pltpu.VMEM((nlat, lat_rows * tracers, lanes), BF16),
+            pltpu.VMEM((nlon * lanes, lanes), BF16),
+            pltpu.VMEM((lat_rows * tracers, nlat * lat_rows * tracers), BF16),
             pltpu.SemaphoreType.DMA,
             pltpu.SemaphoreType.DMA((devices // group,)),
             pltpu.SemaphoreType.DMA((nlon,)),
@@ -516,7 +525,7 @@
         obs_resid,
         obs_cols.reshape(1, nslots),
         obs_owner.reshape(1, blocks),
-        jnp.pad(obs_count, (0, lanes)),
+        obs_count.reshape(1, blocks),
         lon_matrix,
         lat_matrix,
     )

time: 65.7 us -> 61.6 us (0.938)
  Pallas kernels: 60.6 us -> 57.8 us
  local copies, waits for them, and re-layouts: 4.34 us -> 3.06 us
    pallas_call x1, Pallas kernels: 60.6 us -> 57.8 us  [shards(): pl.pallas_call(functools.partial(exchange_kernel, tracers, levels, lat_ro...]
    pad x1 -> x0, local copies, waits for them, and re-layouts: 1.28 us -> none  [shards(): jnp.pad(obs_count, (0, lanes))]
where the time goes in v3:
time: 61.6 us; the launch traced here: 61.5 us
  Pallas kernels  57.8 us (94%)
  local copies, waits for them, and re-layouts  3.06 us (5%)
  between operations  0.65 us (1%)
    pallas_call x1, Pallas kernels, shards(): pl.pallas_call(functools.partial(exchange_kernel, tracers, levels, lat_ro...  57.8 us
    unnamed x4, local copies, waits for them, and re-layouts  3.06 us

profile of v3, /device:TPU:1, one launch (start us, length us, event | category | flops | bytes accessed | tf_op | source)
XLA Modules:
  0.0 61.5 jit_solution(18209047226222505970)
XLA Ops:
  0.6 57.8 %exchange.1 = (f32[2528,128]{1,0:T(8,128)}, f32[4,8,128]{2,1,0:T(8,128)}) custom-call(f32[2528,128]{1,0:T(8,128)} %bitcast.9, bf16[10112,128]{1,0:T(8,128)(2,1)} %bitcast.7, bf16[1264,128]{1,0:T(8,128)(2,1)} %bitcast.10, bf16[79,79]{1,0:T(8,128)(2,1)} %ker_ref.1, bf16[79,4096]{1,0:T(8,128)(2,1)} %w_ref.1, bf16[4,4096]{1,0:T(4,128)(2,1)} %r_ref.1, ...), custom_call_target="tpu_custom_call" | custom-call | tf_op jit(solution)/shard_map/exchange/pallas_call | solution.py:469
  58.4 0.0 copy-start
  58.4 2.4 %copy.15 = f32[4,79,8,128]{3,2,1,0:T(8,128)} copy(f32[4,79,8,128]{3,2,1,0:T(8,128)} %bitcast.8) | data formatting | bytes 2588672
  60.9 0.0 copy-done
  60.9 0.6 copy.16
Async XLA Ops:
  58.4 2.5 %copy-start = (f32[4,8,128]{2,1,0:T(8,128)S(1)}, f32[4,8,128]{2,1,0:T(8,128)}, u32[]{:S(2)}) copy-start(f32[4,8,128]{2,1,0:T(8,128)} %get-tuple-element.9) | copy-start | bytes 49156
